TPU v7x, 32 devices: a whole 2x2x4 slice. The times are simulated.
32 devices in a mesh: groups: 2 (over y), ep: 4 (over z), tp: 4 (over x, core).
Axes of the slice: x: 2, y: 2, z: 4, core: 2. Of those that a mesh axis runs over, the one named last changes fastest.
Arguments:
- tokens: bfloat16 [1024, 2560], P(('groups', 'ep')), parts along dimension 0, may hold values from -6 to 6
- device_choice: int32 [1024, 3], P(('groups', 'ep')), parts along dimension 0, may hold values from 0 to 3, as said below
- local_expert: int32 [1024, 6], P(('groups', 'ep')), parts along dimension 0, may hold values from 0 to 1, as said below
- route_weight: float32 [1024, 6], P(('groups', 'ep')), parts along dimension 0, may hold values from 0.1 to 1
- prefill_ranks: int32 [4], P('groups'), parts along dimension 0, may hold values from 0 to 3, as said below
- w_gate: bfloat16 [8, 1024, 2560], P('ep', 'tp'), may hold values from -0.125 to 0.125
- w_up: bfloat16 [8, 1024, 2560], P('ep', 'tp'), may hold values from -0.125 to 0.125
- w_down: bfloat16 [8, 1024, 2560], P('ep', 'tp'), may hold values from -0.1875 to 0.1875
Outputs:
- moe_out: bfloat16 [1024, 2560], P(('groups', 'ep', 'tp')), parts along dimension 0
There are 2 independent parts, one for each index of `groups`. A program takes and returns all parts, laid end to end along the dimension named above; an argument that names none is the same for every part. Nothing has to cross between parts.
Inputs may be any that keep to these rules, and one draw needn't show every extreme that they name: `device_choice`: each row names 3 different ranks. The rows of one rank (aligned blocks of 128 rows) name any one rank at most 96 times, and every block names some rank exactly 96 times. `local_expert`: picks 2k and 2k + 1 of a row are two different experts of the rank in column k of device_choice. So the rows of one rank choose one expert at most 96 times, and some expert is chosen exactly 96 times by the rows of every rank. `prefill_ranks`: 2 different ranks.
All inputs are finite; a program needn't handle non-finite values.
Results may differ from a plain program's by a relative error of at most 0.014.
Values may be sent and summed in bfloat16 or wider, within the bound.
A program may use at most 128 MiB of HBM per device.

v0:
```python
import functools

import jax
import jax.numpy as jnp
from jax import lax
from jax.experimental import pallas as pl
from jax.experimental.pallas import tpu as pltpu
from jax.sharding import PartitionSpec as P

TOPK = 6
DEV_TOP = 3
DEC_RANK = 8
LANES = 128
CORES = 2
VMEM_BYTES = 67_043_328
CHUNKS = 4
MESH = pl.DeviceIdType.MESH


def count_slots(slot_keys, is_live, bin_count):
    hits = (
        slot_keys[:, :, None] == jnp.arange(bin_count, dtype=jnp.int32)[None, None, :]
    ) & is_live[:, None, None]
    flat_hits = hits.astype(jnp.int32).reshape(-1, bin_count)
    before = jnp.cumsum(flat_hits, axis=0) - flat_hits
    return jnp.sum(before * flat_hits, axis=1).reshape(slot_keys.shape)


def by_collectives(
    tokens, device_choice, local_expert, route_weight, prefill_ranks, w_gate, w_up, w_down
):
    rank_count = lax.axis_size("ep")
    own_rank = lax.axis_index("ep")
    rank_rows = tokens.shape[0]
    model_width = tokens.shape[1]
    experts_here = w_gate.shape[0]
    capacity = (DEV_TOP * rank_rows + rank_count - 1) // rank_count
    row_ids = jnp.arange(rank_rows, dtype=jnp.int32)
    is_live = (row_ids < DEC_RANK) | jnp.any(prefill_ranks == own_rank)
    pair_rank = jnp.repeat(device_choice, 2, axis=1)
    expert_keys = pair_rank * experts_here + local_expert
    positions = count_slots(device_choice, is_live, rank_count)
    send_ids = device_choice * capacity + positions
    send_count = rank_count * capacity
    pick_index = expert_keys * capacity + jnp.repeat(positions, 2, axis=1)
    block_shape = (rank_count, 1, capacity, model_width)
    slot_ids = jnp.arange(send_count, dtype=jnp.int32)
    select = jnp.any(
        (send_ids[None, :, :] == slot_ids[:, None, None]) & is_live[None, :, None], axis=2
    ).astype(jnp.bfloat16)
    outgoing = (
        jnp.dot(select, tokens, preferred_element_type=jnp.float32)
        .astype(jnp.bfloat16)
        .reshape(block_shape)
    )
    blocks = lax.all_to_all(outgoing, "ep", split_axis=0, concat_axis=0, tiled=True)
    gate_act = jnp.einsum("scd,efd->secf", blocks[:, 0], w_gate, preferred_element_type=jnp.float32)
    up_act = jnp.einsum("scd,efd->secf", blocks[:, 0], w_up, preferred_element_type=jnp.float32)
    hidden = (jax.nn.silu(gate_act) * up_act).astype(jnp.bfloat16)
    partial_value = jnp.einsum(
        "secf,efd->secd", hidden, w_down, preferred_element_type=jnp.float32
    ).astype(jnp.bfloat16)
    returned = lax.all_to_all(partial_value, "ep", split_axis=0, concat_axis=0, tiled=True)
    back_width = returned.shape[3]
    flat_back = returned.reshape(-1, back_width)
    weights = jnp.where(is_live[:, None], route_weight, jnp.zeros_like(route_weight))
    shares = jnp.zeros((rank_rows, back_width), jnp.float32)
    for pick_slot in range(TOPK):
        picked_rows = flat_back[pick_index[:, pick_slot]].astype(jnp.float32)
        shares = shares + weights[:, pick_slot : pick_slot + 1] * picked_rows
    summed = lax.psum_scatter(shares.astype(jnp.bfloat16), "tp", scatter_dimension=0, tiled=True)
    return summed


def fused_kernel(
    pairs, cuts, chunks, tokens, choice_in, local_in, route_in, prefill_in, w_gate, w_up, w_down, out,
    raw, slot_rows, mix, gate, up, down, choice, local, route, prefill, total, half_out, half_in,
    side_out, side_in, path_out, near_in, over_in, back_out,
    load_sem, mix_near, mix_over, mix_recv, near_send, over_send, raw_recv, give_send, slot_recv,
    x_send, x_recv, c_send, c_recv, extra_give, extra_recv, extra_x, extra_xr, extra_c, extra_cr,
    half_send, half_recv, side_send, side_recv, path_send, near_recv, over_recv, back_send,
):
    ranks, piece_rows, width = raw.shape
    me = lax.axis_index("ep")
    spot = lax.axis_index("tp")
    column, core = spot // CORES, spot % CORES
    partner = column * CORES + (1 - core)
    across = (1 - column) * CORES + core
    experts, hidden_here, _ = w_gate.shape
    pieces = pairs * CORES
    rank_rows = pieces * piece_rows
    long_piece = piece_rows + DEC_RANK
    chunk_rows = piece_rows // chunks
    parts = range(len(cuts))

    upper = me >= ranks // 2
    end = (me == 0) | (me == ranks - 1)
    inner = ~end
    lead = spot == 0
    relay = (spot == CORES)

    def flip(k):
        return jnp.where(upper, k, ranks - 1 - k)

    place = flip(me)
    near = flip(jnp.where(end, 2, 3))
    over = flip(1)

    loads = [
        pltpu.make_async_copy(tokens.at[spot], raw.at[me], load_sem.at[0]),
        pltpu.make_async_copy(choice_in, choice, load_sem.at[1]),
        pltpu.make_async_copy(local_in, local, load_sem.at[2]),
        pltpu.make_async_copy(route_in, route, load_sem.at[3]),
        pltpu.make_async_copy(prefill_in, prefill, load_sem.at[4]),
        pltpu.make_async_copy(w_gate, gate, load_sem.at[5]),
        pltpu.make_async_copy(w_up, up, load_sem.at[6]),
        pltpu.make_async_copy(w_down, down, load_sem.at[7]),
    ]
    barrier = pltpu.get_barrier_semaphore()
    pl.semaphore_signal(barrier, inc=1, device_id={"ep": near}, device_id_type=MESH)
    pl.semaphore_signal(barrier, inc=1, device_id={"tp": across}, device_id_type=MESH)
    pl.semaphore_signal(barrier, inc=1, device_id={"tp": partner}, device_id_type=MESH)

    @pl.when(inner)
    def _():
        pl.semaphore_signal(barrier, inc=1, device_id={"ep": over}, device_id_type=MESH)

    for load in loads:
        load.start()
    for load in loads[1:5]:
        load.wait()

    hit = jnp.int32(0)
    for j in range(prefill.shape[0]):
        hit = hit + jnp.where(prefill[j] == me, 1, 0)
    table = (mix.shape[1], rank_rows)
    expert_ids = lax.broadcasted_iota(jnp.int32, table, 0)
    row_ids = lax.broadcasted_iota(jnp.int32, table, 1)
    by_expert = jnp.zeros(table, jnp.float32)
    for pick in range(TOPK):
        chosen = choice[pick // 2 : pick // 2 + 1, :] * experts + local[pick : pick + 1, :]
        by_expert = by_expert + jnp.where(expert_ids == chosen, route[pick : pick + 1, :], 0.0)
    mix[me] = jnp.where(row_ids < jnp.where(hit > 0, rank_rows, DEC_RANK), by_expert, 0.0)

    first = flip(prefill[0])
    second = flip(prefill[1])
    high, low = jnp.maximum(first, second), jnp.minimum(first, second)
    idle_high = jnp.where(high != 3, 3, jnp.where(low != 2, 2, 1))
    idle_low = 6 - high - low - idle_high
    live = [high, low]
    idle = [idle_high, idle_low]
    loads[0].wait()

    @pl.when(end)
    def _():
        pl.semaphore_wait(barrier, 3)

    @pl.when(inner)
    def _():
        pl.semaphore_wait(barrier, 4)

    def remote(src, dst, send, recv, target):
        return pltpu.make_async_remote_copy(
            src_ref=src, dst_ref=dst, send_sem=send, recv_sem=recv,
            device_id=target, device_id_type=MESH,
        )

    def columns(part):
        start, size = cuts[part]
        return pl.ds(start, size)

    def mix_to_near(block):
        return remote(mix.at[block], mix.at[block], mix_near.at[block], mix_recv.at[block], {"ep": near})

    def mix_to_over(block):
        return remote(mix.at[block], mix.at[block], mix_over.at[block], mix_recv.at[block], {"ep": over})

    def lines(c):
        return pl.ds(c * chunk_rows, chunk_rows)

    def to_near(block, c):
        piece = raw.at[block, lines(c)]
        return remote(piece, piece, near_send.at[c], raw_recv.at[block, c], {"ep": near})

    def to_over(block, c):
        piece = raw.at[block, lines(c)]
        return remote(piece, piece, over_send.at[block, c], raw_recv.at[block, c], {"ep": over})

    def slot_chunk(slot, holder, c):
        start = pl.multiple_of(holder * piece_rows + c * chunk_rows, chunk_rows)
        return slot_rows.at[slot, pl.ds(start, chunk_rows)]

    def slot_extra(slot):
        return slot_rows.at[slot, pl.ds(rank_rows, DEC_RANK)]

    def give(slot, c):
        piece = slot_chunk(slot, spot, c)
        return remote(piece, piece, give_send.at[slot, c], slot_recv.at[slot, c], {"ep": near})

    def give_extra(slot):
        piece = slot_extra(slot)
        return remote(piece, piece, extra_give.at[slot], extra_recv.at[slot], {"ep": near})

    def x_copy(slot, c):
        piece = slot_chunk(slot, spot, c)
        return remote(piece, piece, x_send.at[slot, c], x_recv.at[slot, c], {"tp": across})

    def x_extra(slot):
        piece = slot_extra(slot)
        return remote(piece, piece, extra_x.at[slot], extra_xr.at[slot], {"tp": across})

    def c_copy(slot, step, c):
        piece = slot_chunk(slot, across if step else spot, c)
        return remote(piece, piece, c_send.at[slot, step, c], c_recv.at[slot, step, c], {"tp": partner})

    def c_extra(slot):
        piece = slot_extra(slot)
        return remote(piece, piece, extra_c.at[slot], extra_cr.at[slot], {"tp": partner})

    def half_copy(slot, part):
        cols = columns(part)
        return remote(
            half_out.at[slot, :, :, cols], half_in.at[slot, :, :, cols],
            half_send.at[slot, part], half_recv.at[slot, part], {"tp": partner},
        )

    def either(long_here, make, act):
        @pl.when(long_here)
        def _():
            act(make(long_piece))

        @pl.when(~long_here)
        def _():
            act(make(piece_rows))

    def start(copy):
        copy.start()

    def wait_send(copy):
        copy.wait_send()

    def wait_recv(copy):
        copy.wait_recv()

    def side_copy(slot, part):
        cols = columns(part)
        return lambda rows: remote(
            side_out.at[slot, pl.ds(0, rows), cols], side_in.at[slot, pl.ds(0, rows), cols],
            side_send.at[slot, part], side_recv.at[slot, part], {"tp": across},
        )

    def inward(slot, part):
        cols = columns(part)
        return lambda rows: remote(
            path_out.at[slot, pl.ds(0, rows), cols], near_in.at[slot, pl.ds(0, rows), cols],
            path_send.at[slot, part], near_recv.at[slot, part], {"ep": near},
        )

    def crossing(slot, part):
        cols = columns(part)
        return lambda rows: remote(
            path_out.at[slot, pl.ds(0, rows), cols], over_in.at[1 - slot, pl.ds(0, rows), cols],
            path_send.at[slot, part], over_recv.at[1 - slot, part], {"ep": over},
        )

    def backward(part):
        cols = columns(part)
        return lambda rows: remote(
            back_out.at[pl.ds(0, rows), cols], near_in.at[0, pl.ds(0, rows), cols],
            back_send.at[part], near_recv.at[0, part], {"ep": near},
        )

    def choose(slot, which, get):
        candidates = (1, 2, 3) if slot == 0 else (0, 1, 2)
        value = get(flip(candidates[0]))
        for k in candidates[1:]:
            value = lax.select(which == k, get(flip(k)), value)
        return value

    def slot_arrive(slot, c):
        at = pl.multiple_of(spot * piece_rows + c * chunk_rows, chunk_rows)

        @pl.when(end)
        def _():
            give(slot, c).wait_recv()

        @pl.when(inner)
        def _():
            if slot == 0:
                to_near(flip(3), c).wait_recv()
                to_over(flip(3), c).start()
                to_over(flip(1), c).wait_recv()
            else:
                to_over(flip(0), c).wait_recv()
            slot_rows[slot, pl.ds(at, chunk_rows), :] = choose(
                slot, live[slot], lambda block: raw[block, lines(c), :]
            )
            give(slot, c).start()

        x_copy(slot, c).start()
        c_copy(slot, 0, c).start()
        if c == 0:
            @pl.when(lead)
            def _():
                @pl.when(end)
                def _():
                    give_extra(slot).wait_recv()

                @pl.when(inner)
                def _():
                    slot_rows[slot, pl.ds(rank_rows, DEC_RANK), :] = choose(
                        slot, idle[slot], lambda block: raw[block, 0:DEC_RANK, :]
                    )
                    give_extra(slot).start()

                x_extra(slot).start()
                c_extra(slot).start()

    def x_arrive(slot, c):
        x_copy(slot, c).wait_recv()
        c_copy(slot, 1, c).start()
        if c == 0:
            @pl.when(relay)
            def _():
                x_extra(slot).wait_recv()
                c_extra(slot).start()

    def all_here(slot):
        for c in range(chunks):
            for step in range(2):
                c_copy(slot, step, c).wait_recv()

        @pl.when(core == 1)
        def _():
            c_extra(slot).wait_recv()

    def mix_arrive(k):
        at_end, inside = 2 - k, (1, 3, 0)[k]
        block = flip(jnp.where(end, at_end, inside))
        mix_to_near(block).wait_recv()

        @pl.when(inner)
        def _():
            if inside == 3:
                mix_to_over(block).start()
            else:
                mix_to_near(block).start()

    def compute(slot):
        rows = slot_rows[slot]
        hidden = []
        for expert in range(experts):
            by_row = (((1,), (1,)), ((), ()))
            gate_act = lax.dot_general(rows, gate[expert], by_row, preferred_element_type=jnp.float32)
            up_act = lax.dot_general(rows, up[expert], by_row, preferred_element_type=jnp.float32)

            def weights(which):
                line = choose(slot, which, lambda block: mix[block, pl.ds(me * experts + expert, 1), :])
                return jnp.broadcast_to(line, (LANES, rank_rows)).T

            scale = jnp.concatenate([weights(live[slot]), weights(idle[slot])[0:DEC_RANK]], axis=0)
            scale = jnp.concatenate([scale] * (hidden_here // LANES), axis=1)
            act = gate_act / (1.0 + jnp.exp(-gate_act)) * up_act * scale
            hidden.append(act.astype(jnp.bfloat16))
        hidden = jnp.concatenate(hidden, axis=1)
        for part in parts:
            low_col, size = cuts[part]
            product = jnp.dot(
                hidden,
                down[:, :, low_col:low_col + size].reshape(experts * hidden_here, size),
                preferred_element_type=jnp.float32,
            )
            cols = columns(part)
            total[slot, :, 0:piece_rows, cols] = product[0:rank_rows].reshape(pieces, piece_rows, size)
            for piece in range(pieces):
                total[slot, piece, piece_rows:long_piece, cols] = product[rank_rows:]
            for col in range(pairs):
                half_out[slot, col, :, cols] = total[
                    slot, col * CORES + (1 - core), :, cols
                ].astype(jnp.bfloat16)
            half_copy(slot, part).start()

    def merge_half(slot):
        for part in parts:
            cols = columns(part)
            half_copy(slot, part).wait_recv()
            got = half_in[slot, 1 - column, :, cols].astype(jnp.float32)
            side_out[slot, :, cols] = (total[slot, across, :, cols] + got).astype(jnp.bfloat16)
            either(relay, side_copy(slot, part), start)
            got = half_in[slot, column, :, cols].astype(jnp.float32)
            total[slot, spot, :, cols] = total[slot, spot, :, cols] + got

    def merge_side(slot, part):
        cols = columns(part)
        either(lead, side_copy(slot, part), wait_recv)
        acc = total[slot, spot, :, cols] + side_in[slot, :, cols].astype(jnp.float32)
        total[slot, spot, :, cols] = acc

        @pl.when(end)
        def _():
            path_out[slot, :, cols] = acc.astype(jnp.bfloat16)
            either(lead, inward(slot, part), start)

    def pass_over(slot, part):
        cols = columns(part)

        @pl.when(inner)
        def _():
            either(lead, inward(slot, part), wait_recv)
            acc = total[slot, spot, :, cols] + near_in[slot, :, cols].astype(jnp.float32)
            path_out[slot, :, cols] = acc.astype(jnp.bfloat16)
            either(lead, crossing(slot, part), start)

    mix_to_near(me).start()

    @pl.when(end)
    def _():
        for c in range(chunks):
            to_near(me, c).start()

    @pl.when(inner)
    def _():
        mix_to_over(me).start()
        for c in range(chunks):
            to_over(me, c).start()

    for c in range(chunks):
        slot_arrive(0, c)
        if c == 0:
            mix_arrive(0)
    mix_arrive(1)
    for c in range(chunks):
        x_arrive(0, c)
        slot_arrive(1, c)
    mix_arrive(2)
    for load in loads[5:]:
        load.wait()
    all_here(0)
    compute(0)
    for c in range(chunks):
        x_arrive(1, c)
    merge_half(0)
    all_here(1)
    compute(1)
    for part in parts:
        merge_side(0, part)
    merge_half(1)
    for part in parts:
        pass_over(0, part)
    for part in parts:
        merge_side(1, part)
        pass_over(1, part)

    def finish(part, tops, lows):
        cols = columns(part)
        is_high, is_low = high == place, low == place
        zero = jnp.zeros((piece_rows, cuts[part][1]), jnp.float32)
        body = lax.select(is_high, tops[0:piece_rows], zero)
        rest = lax.select(idle_high == place, tops[piece_rows:long_piece], zero[0:DEC_RANK])
        if lows is not None:
            body = lax.select(is_low, lows[0:piece_rows], body)
            rest = lax.select(idle_low == place, lows[piece_rows:long_piece], rest)
        rest = lax.select(lead & ~is_high & ~is_low, rest, body[0:DEC_RANK])
        body = jnp.concatenate([rest, body[DEC_RANK:]], axis=0)
        out[:, cols] = body.astype(out.dtype)

    for part in parts:
        cols = columns(part)

        @pl.when(inner)
        def _():
            either(lead, crossing(1, part), wait_recv)
            crossed = over_in[0, :, cols].astype(jnp.float32)
            mine = total[0, spot, :, cols] + crossed
            back_out[:, cols] = mine.astype(jnp.bfloat16)
            either(lead, backward(part), start)
            either(lead, crossing(0, part), wait_recv)
            tops = mine + near_in[0, :, cols].astype(jnp.float32)
            lows = total[1, spot, :, cols] + near_in[1, :, cols].astype(jnp.float32)
            finish(part, tops, lows + over_in[1, :, cols].astype(jnp.float32))

    for part in parts:
        cols = columns(part)

        @pl.when(end)
        def _():
            either(lead, backward(part), wait_recv)
            finish(part, total[0, spot, :, cols] + near_in[0, :, cols].astype(jnp.float32), None)

    mix_to_near(me).wait_send()

    @pl.when(end)
    def _():
        for c in range(chunks):
            to_near(me, c).wait_send()

    @pl.when(inner)
    def _():
        mix_to_over(me).wait_send()
        mix_to_over(flip(3)).wait_send()
        for k in (1, 0):
            mix_to_near(flip(k)).wait_send()
        for c in range(chunks):
            to_over(me, c).wait_send()
            to_over(flip(3), c).wait_send()
            for slot in range(2):
                give(slot, c).wait_send()
        for part in parts:
            either(lead, backward(part), wait_send)

        @pl.when(lead)
        def _():
            for slot in range(2):
                give_extra(slot).wait_send()

    for slot in range(2):
        for c in range(chunks):
            x_copy(slot, c).wait_send()
            for step in range(2):
                c_copy(slot, step, c).wait_send()

        @pl.when(lead)
        def _():
            x_extra(slot).wait_send()

        @pl.when(core == 0)
        def _():
            c_extra(slot).wait_send()

        for part in parts:
            half_copy(slot, part).wait_send()
            either(relay, side_copy(slot, part), wait_send)
            either(lead, inward(slot, part), wait_send)


def column_cuts(width):
    unit = 512 if width % 512 == 0 else LANES
    return [(low, unit) for low in range(0, width, unit)]


def scratch_of(ranks, pairs, parts, chunks, experts, rank_rows, hidden_here, width):
    pieces = pairs * CORES
    piece_rows = rank_rows // pieces
    long_piece = piece_rows + DEC_RANK
    sub = (ranks * experts + 7) // 8 * 8
    arrays = [
        ((ranks, piece_rows, width), jnp.bfloat16),
        ((2, rank_rows + DEC_RANK, width), jnp.bfloat16),
        ((ranks, sub, rank_rows), jnp.float32),
        ((experts, hidden_here, width), jnp.bfloat16),
        ((experts, hidden_here, width), jnp.bfloat16),
        ((experts, hidden_here, width), jnp.bfloat16),
        ((DEV_TOP, rank_rows), jnp.int32),
        ((TOPK, rank_rows), jnp.int32),
        ((TOPK, rank_rows), jnp.float32),
        None,
        ((2, pieces, long_piece, width), jnp.float32),
        ((2, pairs, long_piece, width), jnp.bfloat16),
        ((2, pairs, long_piece, width), jnp.bfloat16),
        ((2, long_piece, width), jnp.bfloat16),
        ((2, long_piece, width), jnp.bfloat16),
        ((2, long_piece, width), jnp.bfloat16),
        ((2, long_piece, width), jnp.bfloat16),
        ((2, long_piece, width), jnp.bfloat16),
        ((long_piece, width), jnp.bfloat16),
    ]
    sems = [
        (8,), (ranks,), (ranks,), (ranks,),
        (chunks,), (ranks, chunks), (ranks, chunks), (2, chunks), (2, chunks),
        (2, chunks), (2, chunks), (2, 2, chunks), (2, 2, chunks),
        (2,), (2,), (2,), (2,), (2,), (2,),
        (2, parts), (2, parts), (2, parts), (2, parts), (2, parts), (2, parts), (2, parts), (parts,),
    ]
    return arrays, sems


def byte_count(arrays):
    total = 0
    for shape, kind in filter(None, arrays):
        size = jnp.dtype(kind).itemsize
        for extent in shape:
            size *= extent
        total += size
    return total


def on_device(
    tokens, device_choice, local_expert, route_weight, prefill_ranks, w_gate, w_up, w_down
):
    ranks = lax.axis_size("ep")
    spots = lax.axis_size("tp")
    rank_rows, width = tokens.shape
    experts, hidden_here, _ = w_gate.shape
    pairs = spots // CORES
    fits = False
    if (
        ranks == 4 and pairs == 2 and spots % CORES == 0 and prefill_ranks.shape[0] == 2
        and rank_rows == LANES and ranks * experts <= LANES and hidden_here % LANES == 0 and width % LANES == 0
    ):
        cuts = column_cuts(width)
        arrays, sems = scratch_of(
            ranks, pairs, len(cuts), CHUNKS, experts, rank_rows, hidden_here, width
        )
        fits = byte_count(arrays) < VMEM_BYTES * 3 // 4
    if not fits:
        return by_collectives(
            tokens, device_choice, local_expert, route_weight, prefill_ranks, w_gate, w_up, w_down
        )
    piece_rows = rank_rows // spots
    anywhere = pl.BlockSpec(memory_space=pl.ANY)
    in_vmem = pl.BlockSpec(memory_space=pltpu.VMEM)
    return pl.pallas_call(
        functools.partial(fused_kernel, pairs, cuts, CHUNKS),
        out_shape=jax.ShapeDtypeStruct((piece_rows, width), jnp.bfloat16),
        in_specs=[anywhere] * 8,
        out_specs=in_vmem,
        scratch_shapes=[pltpu.VMEM(*spec) if spec else pltpu.SMEM((2,), jnp.int32) for spec in arrays]
        + [pltpu.SemaphoreType.DMA(shape) for shape in sems],
        compiler_params=pltpu.CompilerParams(
            collective_id=0, has_side_effects=True, vmem_limit_bytes=VMEM_BYTES * 15 // 16
        ),
    )(
        tokens.reshape(spots, piece_rows, width), device_choice.T, local_expert.T,
        route_weight.T, prefill_ranks, w_gate, w_up, w_down,
    )


def solution(mesh):
    in_specs = (
        P(("groups", "ep"), None),
        P(("groups", "ep"), None),
        P(("groups", "ep"), None),
        P(("groups", "ep"), None),
        P("groups"),
        P("ep", "tp", None),
        P("ep", "tp", None),
        P("ep", "tp", None),
    )
    out_specs = P(("groups", "ep", "tp"), None)
    return jax.shard_map(
        on_device, mesh=mesh, in_specs=in_specs, out_specs=out_specs, check_vma=False
    )
```

profile of v0, /device:TPU:0, one launch (start us, length us, event | category | flops | bytes accessed | tf_op | source)
XLA Modules:
  0.0 46.2 jit_solution(5354514808410795112)
XLA Ops:
  0.0 44.6 %shard_map.82 = bf16[32,2560]{1,0:T(8,128)(2,1)} custom-call(bf16[4,32,2560]{2,1,0:T(8,128)(2,1)} %bitcast.4, s32[3,128]{1,0:T(4,128)} %bitcast.7, s32[6,128]{1,0:T(8,128)} %bitcast.5, f32[6,128]{1,0:T(8,128)} %bitcast.6, s32[2]{0:T(128)} %prefill_in.1, bf16[2,256,2560]{2,1,0:T(8,128)(2,1)} %w_gate.1, bf16[2,256,2560]{2,1,0:T(8,128)(2,1)} %w_up.1, ...), custom_call_target="tpu_custom_call" | custom-call | tf_op jit(solution)/shard_map/pallas_call | solution.py:612
  44.6 1.6 %copy.10 = bf16[32,2560]{1,0:T(8,128)(2,1)} copy(bf16[32,2560]{1,0:T(8,128)(2,1)} %shard_map.82) | data formatting | bytes 327680
where the time goes:
time: 46.3 us; the launch traced here: 46.2 us
  Pallas kernels  44.6 us (96%)
  local copies, waits for them, and re-layouts  1.59 us (3%)
    pallas_call x1, Pallas kernels, on_device(): pl.pallas_call(functools.partial(fused_kernel, pairs, cuts, CHUNKS), out_...  44.6 us
    unnamed x1, local copies, waits for them, and re-layouts  1.59 us

commit v1 on v0

--- a/solution.py
+++ b/solution.py
@@ -74,11 +74,11 @@
 
 def fused_kernel(
     pairs, cuts, chunks, tokens, choice_in, local_in, route_in, prefill_in, w_gate, w_up, w_down, out,
-    raw, slot_rows, mix, gate, up, down, choice, local, route, prefill, total, half_out, half_in,
-    side_out, side_in, path_out, near_in, over_in, back_out,
+    raw, slot_rows, mix, gate, up, gate_t, up_t, down, choice, local, route, prefill, total, half_out, half_in,
+    side_out, side_in, path_out, near_in, over_in, far_in, back_out,
     load_sem, mix_near, mix_over, mix_recv, near_send, over_send, raw_recv, give_send, slot_recv,
     x_send, x_recv, c_send, c_recv, extra_give, extra_recv, extra_x, extra_xr, extra_c, extra_cr,
-    half_send, half_recv, side_send, side_recv, path_send, near_recv, over_recv, back_send,
+    half_send, half_recv, side_send, side_recv, path_send, near_recv, over_recv, far_send, far_recv, back_send,
 ):
     ranks, piece_rows, width = raw.shape
     me = lax.axis_index("ep")
@@ -121,9 +121,11 @@
     pl.semaphore_signal(barrier, inc=1, device_id={"tp": across}, device_id_type=MESH)
     pl.semaphore_signal(barrier, inc=1, device_id={"tp": partner}, device_id_type=MESH)
 
+    pl.semaphore_signal(barrier, inc=1, device_id={"ep": over}, device_id_type=MESH)
+
     @pl.when(inner)
     def _():
-        pl.semaphore_signal(barrier, inc=1, device_id={"ep": over}, device_id_type=MESH)
+        pl.semaphore_signal(barrier, inc=1, device_id={"ep": flip(0)}, device_id_type=MESH)
 
     for load in loads:
         load.start()
@@ -153,11 +155,11 @@
 
     @pl.when(end)
     def _():
-        pl.semaphore_wait(barrier, 3)
+        pl.semaphore_wait(barrier, 4)
 
     @pl.when(inner)
     def _():
-        pl.semaphore_wait(barrier, 4)
+        pl.semaphore_wait(barrier, 5)
 
     def remote(src, dst, send, recv, target):
         return pltpu.make_async_remote_copy(
@@ -261,6 +263,13 @@
         return lambda rows: remote(
             path_out.at[slot, pl.ds(0, rows), cols], over_in.at[1 - slot, pl.ds(0, rows), cols],
             path_send.at[slot, part], over_recv.at[1 - slot, part], {"ep": over},
+        )
+
+    def direct(part):
+        cols = columns(part)
+        return lambda rows: remote(
+            path_out.at[1, pl.ds(0, rows), cols], far_in.at[pl.ds(0, rows), cols],
+            far_send.at[part], far_recv.at[part], {"ep": over},
         )
 
     def backward(part):
@@ -350,9 +359,8 @@
         rows = slot_rows[slot]
         hidden = []
         for expert in range(experts):
-            by_row = (((1,), (1,)), ((), ()))
-            gate_act = lax.dot_general(rows, gate[expert], by_row, preferred_element_type=jnp.float32)
-            up_act = lax.dot_general(rows, up[expert], by_row, preferred_element_type=jnp.float32)
+            gate_act = jnp.dot(rows, gate_t[expert], preferred_element_type=jnp.float32)
+            up_act = jnp.dot(rows, up_t[expert], preferred_element_type=jnp.float32)
 
             def weights(which):
                 line = choose(slot, which, lambda block: mix[block, pl.ds(me * experts + expert, 1), :])
@@ -396,10 +404,21 @@
         acc = total[slot, spot, :, cols] + side_in[slot, :, cols].astype(jnp.float32)
         total[slot, spot, :, cols] = acc
 
-        @pl.when(end)
-        def _():
+        if slot == 1:
             path_out[slot, :, cols] = acc.astype(jnp.bfloat16)
-            either(lead, inward(slot, part), start)
+
+            @pl.when(end)
+            def _():
+                either(lead, direct(part), start)
+
+            @pl.when(inner)
+            def _():
+                either(lead, crossing(slot, part), start)
+        else:
+            @pl.when(end)
+            def _():
+                path_out[slot, :, cols] = acc.astype(jnp.bfloat16)
+                either(lead, inward(slot, part), start)
 
     def pass_over(slot, part):
         cols = columns(part)
@@ -424,6 +443,11 @@
         for c in range(chunks):
             to_over(me, c).start()
 
+    for load in loads[5:]:
+        load.wait()
+    for expert in range(experts):
+        gate_t[expert] = gate[expert].T
+        up_t[expert] = up[expert].T
     for c in range(chunks):
         slot_arrive(0, c)
         if c == 0:
@@ -433,8 +457,6 @@
         x_arrive(0, c)
         slot_arrive(1, c)
     mix_arrive(2)
-    for load in loads[5:]:
-        load.wait()
     all_here(0)
     compute(0)
     for c in range(chunks):
@@ -442,14 +464,19 @@
     merge_half(0)
     all_here(1)
     compute(1)
+    merge_half(1)
     for part in parts:
         merge_side(0, part)
-    merge_half(1)
+    for part in parts:
+        merge_side(1, part)
+
+    @pl.when(end)
+    def _():
+        for part in parts:
+            either(lead, inward(1, part), start)
+
     for part in parts:
         pass_over(0, part)
-    for part in parts:
-        merge_side(1, part)
-        pass_over(1, part)
 
     def finish(part, tops, lows):
         cols = columns(part)
@@ -464,26 +491,29 @@
         body = jnp.concatenate([rest, body[DEC_RANK:]], axis=0)
         out[:, cols] = body.astype(out.dtype)
 
-    for part in parts:
-        cols = columns(part)
-
-        @pl.when(inner)
-        def _():
+    @pl.when(inner)
+    def _():
+        for part in parts:
+            cols = columns(part)
             either(lead, crossing(1, part), wait_recv)
-            crossed = over_in[0, :, cols].astype(jnp.float32)
-            mine = total[0, spot, :, cols] + crossed
+            either(lead, direct(part), wait_recv)
+            mine = total[0, spot, :, cols] + over_in[0, :, cols].astype(jnp.float32)
+            mine = mine + far_in[:, cols].astype(jnp.float32)
             back_out[:, cols] = mine.astype(jnp.bfloat16)
             either(lead, backward(part), start)
+            total[0, spot, :, cols] = mine
+        for part in parts:
+            cols = columns(part)
             either(lead, crossing(0, part), wait_recv)
-            tops = mine + near_in[0, :, cols].astype(jnp.float32)
+            either(lead, inward(1, part), wait_recv)
+            tops = total[0, spot, :, cols] + near_in[0, :, cols].astype(jnp.float32)
             lows = total[1, spot, :, cols] + near_in[1, :, cols].astype(jnp.float32)
             finish(part, tops, lows + over_in[1, :, cols].astype(jnp.float32))
 
-    for part in parts:
-        cols = columns(part)
-
-        @pl.when(end)
-        def _():
+    @pl.when(end)
+    def _():
+        for part in parts:
+            cols = columns(part)
             either(lead, backward(part), wait_recv)
             finish(part, total[0, spot, :, cols] + near_in[0, :, cols].astype(jnp.float32), None)
 
@@ -493,6 +523,8 @@
     def _():
         for c in range(chunks):
             to_near(me, c).wait_send()
+        for part in parts:
+            either(lead, direct(part), wait_send)
 
     @pl.when(inner)
     def _():
@@ -549,6 +581,8 @@
         ((ranks, sub, rank_rows), jnp.float32),
         ((experts, hidden_here, width), jnp.bfloat16),
         ((experts, hidden_here, width), jnp.bfloat16),
+        ((experts, width, hidden_here), jnp.bfloat16),
+        ((experts, width, hidden_here), jnp.bfloat16),
         ((experts, hidden_here, width), jnp.bfloat16),
         ((DEV_TOP, rank_rows), jnp.int32),
         ((TOPK, rank_rows), jnp.int32),
@@ -563,13 +597,14 @@
         ((2, long_piece, width), jnp.bfloat16),
         ((2, long_piece, width), jnp.bfloat16),
         ((long_piece, width), jnp.bfloat16),
+        ((long_piece, width), jnp.bfloat16),
     ]
     sems = [
         (8,), (ranks,), (ranks,), (ranks,),
         (chunks,), (ranks, chunks), (ranks, chunks), (2, chunks), (2, chunks),
         (2, chunks), (2, chunks), (2, 2, chunks), (2, 2, chunks),
         (2,), (2,), (2,), (2,), (2,), (2,),
-        (2, parts), (2, parts), (2, parts), (2, parts), (2, parts), (2, parts), (2, parts), (parts,),
+        (2, parts), (2, parts), (2, parts), (2, parts), (2, parts), (2, parts), (2, parts), (parts,), (parts,), (parts,),
     ]
     return arrays, sems
 

time: 46.3 us -> 44.1 us (0.952)
  Pallas kernels: 44.6 us -> 42.3 us
    pallas_call x1, Pallas kernels: 44.6 us -> 42.3 us  [on_device(): pl.pallas_call(functools.partial(fused_kernel, pairs, cuts, CHUNKS), out_...]
where the time goes in v1:
time: 44.1 us; the launch traced here: 43.9 us
  Pallas kernels  42.3 us (96%)
  local copies, waits for them, and re-layouts  1.59 us (4%)
    pallas_call x1, Pallas kernels, on_device(): pl.pallas_call(functools.partial(fused_kernel, pairs, cuts, CHUNKS), out_...  42.3 us
    unnamed x1, local copies, waits for them, and re-layouts  1.59 us

profile of v1, /device:TPU:0, one launch (start us, length us, event | category | flops | bytes accessed | tf_op | source)
XLA Modules:
  0.0 43.9 jit_solution(14126329802537149346)
XLA Ops:
  0.0 42.3 %shard_map.82 = bf16[32,2560]{1,0:T(8,128)(2,1)} custom-call(bf16[4,32,2560]{2,1,0:T(8,128)(2,1)} %bitcast.4, s32[3,128]{1,0:T(4,128)} %bitcast.7, s32[6,128]{1,0:T(8,128)} %bitcast.5, f32[6,128]{1,0:T(8,128)} %bitcast.6, s32[2]{0:T(128)} %prefill_in.1, bf16[2,256,2560]{2,1,0:T(8,128)(2,1)} %w_gate.1, bf16[2,256,2560]{2,1,0:T(8,128)(2,1)} %w_up.1, ...), custom_call_target="tpu_custom_call" | custom-call | tf_op jit(solution)/shard_map/pallas_call | solution.py:647
  42.3 1.6 %copy.10 = bf16[32,2560]{1,0:T(8,128)(2,1)} copy(bf16[32,2560]{1,0:T(8,128)(2,1)} %shard_map.82) | data formatting | bytes 327680
